TPU v7x, 32 devices: a whole 2x2x4 slice. The times are simulated.
32 devices in a mesh: dp: 16 (over z, y, core), expert: 2 (over x).
Axes of the slice: x: 2, y: 2, z: 4, core: 2. Of those that a mesh axis runs over, the one named last changes fastest.
Arguments:
- tokens: bfloat16 [256, 6144], P(('dp', 'expert')), may hold values from -6 to 6
- router_now: float32 [6144, 8], P('dp'), may hold values from -0.078125 to 0.078125
- router_next: float32 [6144, 8], P('dp'), may hold values from -0.078125 to 0.078125
- w_gate: bfloat16 [8, 6144, 8192], P('expert', None, 'dp'), may hold values from -0.078125 to 0.078125
- w_up: bfloat16 [8, 6144, 8192], P('expert', None, 'dp'), may hold values from -0.078125 to 0.078125
- w_down: bfloat16 [8, 8192, 6144], P('expert', 'dp'), may hold values from -0.0625 to 0.0625
- expert_ids: int32 [256, 2], P(('dp', 'expert')), may hold values from 0 to 7, all different within a row; in each aligned block of 8 rows (0 to 7, 8 to 15, ...) at most 4 rows name the same one
- next_ids: int32 [256, 2], P(('dp', 'expert')), may hold values from 0 to 7, all different within a row
Outputs:
- layer_out: bfloat16 [256, 6144], P(('dp', 'expert'))
- next_logits: float32 [256, 8], P(('dp', 'expert'))
- next_weights: float32 [256, 2], P(('dp', 'expert'))
Inputs may be any that keep to these rules, and one draw needn't show every extreme that they name: `expert_ids`: each row names 2 different experts. Among the 8 rows of one device no expert is named by more than 4 rows, and on some devices one expert is named by exactly 4 rows. `next_ids`: each row names 2 different experts.
All inputs are finite; a program needn't handle non-finite values.
Results may differ from a plain program's by a relative error of at most 0.013.
Values may be sent and summed in bfloat16 or wider, within the bound.
A program may use at most 128 MiB of HBM per device.

v0:
```python
import jax
import jax.numpy as jnp
from jax import lax
from jax.sharding import PartitionSpec as P

CAP = 4


epsilon = 1e-05


def rms_normed(values):
    return values * lax.rsqrt(jnp.mean(values * values, axis=-1, keepdims=True) + epsilon)


def pair_weights(logits, chosen):
    picked = jnp.take_along_axis(logits, chosen, axis=1)
    first = jax.nn.sigmoid(picked[:, 0] - picked[:, 1])
    return jnp.stack([first, 1.0 - first], axis=1)


def on_device(tokens, router_now, router_next, w_gate, w_up, w_down, expert_ids, next_ids):
    whole_now, whole_next = (
        lax.all_gather(router_now, "dp", axis=0, tiled=True),
        lax.all_gather(router_next, "dp", axis=0, tiled=True),
    )
    resid = tokens.astype(jnp.float32)
    normed = rms_normed(resid)
    logits = jnp.dot(
        normed, whole_now, precision=lax.Precision.HIGHEST, preferred_element_type=jnp.float32
    )
    weights = pair_weights(logits, expert_ids)
    rounded = normed.astype(jnp.bfloat16)
    expert_count = whole_now.shape[1]
    per_device = w_gate.shape[0]
    groups = lax.axis_size("expert")
    tok_count = tokens.shape[0]
    top_count = expert_ids.shape[1]
    width = tokens.shape[1]
    pairs = tok_count * top_count
    chosen = expert_ids.reshape(pairs)
    onehot = (chosen[:, None] == jnp.arange(expert_count, dtype=jnp.int32)[None, :]).astype(
        jnp.int32
    )
    ranks = jnp.sum((jnp.cumsum(onehot, axis=0) - onehot) * onehot, axis=1)
    places = chosen * CAP + ranks
    place_table = (
        places[:, None] == jnp.arange(expert_count * CAP, dtype=jnp.int32)[None, :]
    ).astype(jnp.float32)
    owners = (
        (jnp.arange(pairs, dtype=jnp.int32) // top_count)[:, None]
        == jnp.arange(tok_count, dtype=jnp.int32)[None, :]
    ).astype(jnp.float32)
    sender = jnp.dot(place_table.T, owners, preferred_element_type=jnp.float32)
    dispatched = jnp.dot(
        sender.astype(jnp.bfloat16), rounded, preferred_element_type=jnp.float32
    ).astype(jnp.bfloat16)
    dispatched = dispatched.reshape(groups, per_device, CAP, width)
    received = lax.all_to_all(dispatched, "expert", split_axis=0, concat_axis=0, tiled=True)
    combine = jnp.sum(
        (place_table * weights.reshape(pairs)[:, None]).reshape(
            tok_count, top_count, expert_count * CAP
        ),
        axis=1,
    )
    hidden_list = []
    for local in range(per_device):
        arriving = received[:, local].reshape(groups * CAP, width)

        def activate(piece, start, local=local):
            gate = jnp.dot(piece, w_gate[local], preferred_element_type=jnp.float32)
            upward = jnp.dot(piece, w_up[local], preferred_element_type=jnp.float32)
            return (jax.nn.silu(gate) * upward).astype(jnp.bfloat16)

        hidden_list.append(
            activate(lax.all_gather(arriving, "dp", axis=0, tiled=True), jnp.int32(0))
        )
    partial_list = []
    for local in range(per_device):
        full = jnp.dot(hidden_list[local], w_down[local], preferred_element_type=jnp.float32)
        partial_list.append(full.reshape(-1, groups, CAP, width))
    stacked = jnp.stack(partial_list, axis=2)
    back = lax.all_to_all(
        stacked.astype(jnp.bfloat16), "expert", split_axis=1, concat_axis=1, tiled=True
    ).astype(stacked.dtype)
    rows_dp = back.shape[0]
    back = back.reshape(rows_dp, expert_count * CAP, width)
    column_table = lax.all_gather(combine, "dp", axis=0, tiled=True).reshape(
        rows_dp, tok_count, expert_count * CAP
    )
    token_terms = jnp.einsum("itc,icd->itd", column_table, back, precision=lax.Precision.HIGHEST)
    mixture = lax.psum_scatter(
        token_terms.reshape(rows_dp * tok_count, width).astype(jnp.bfloat16),
        "dp",
        scatter_dimension=0,
        tiled=True,
    ).astype(jnp.float32)
    summed = resid + mixture
    layer_out = summed.astype(jnp.bfloat16)
    next_logits = jnp.dot(
        rms_normed(summed),
        whole_next,
        precision=lax.Precision.HIGHEST,
        preferred_element_type=jnp.float32,
    )
    next_weights = pair_weights(next_logits, next_ids)
    return (layer_out, next_logits, next_weights)


def solution(mesh):
    in_specs = (
        P(("dp", "expert"), None),
        P("dp", None),
        P("dp", None),
        P("expert", None, "dp"),
        P("expert", None, "dp"),
        P("expert", "dp", None),
        P(("dp", "expert"), None),
        P(("dp", "expert"), None),
    )
    out_specs = (P(("dp", "expert"), None), P(("dp", "expert"), None), P(("dp", "expert"), None))
    return jax.shard_map(
        on_device, mesh=mesh, in_specs=in_specs, out_specs=out_specs, check_vma=False
    )
```

profile of v0, /device:TPU:0, one launch (start us, length us, event | category | flops | bytes accessed | tf_op | source)
XLA Modules:
  0.0 360.8 jit_solution(3658949712199353522)
XLA Ops:
  7.2 0.8 copy.70
  8.0 0.1 eq.48
  8.0 0.1 fusion.77
  8.2 0.2 select_reduce_fusion.1
  8.4 1.1 fusion.64
  9.4 1.4 convolution_convert_fusion.5
  10.9 0.1 reshape.109
  11.0 10.6 %all_to_all.10 = bf16[2,4,4,6144]{3,2,1,0:T(4,128)(2,1)S(1)} all-to-all(bf16[2,4,4,6144]{3,2,1,0:T(4,128)(2,1)S(1)} %reshape.109), channel_id=1, replica_groups=mesh['dp'=16,'expert'=2] {'expert'}, dimensions={0} | all-to-all | bytes 786432 | tf_op jit(solution)/shard_map/all_to_all | solution.py:59
  21.6 0.1 fusion.82
  21.8 0.7 reshape_squeeze.12
  22.5 0.0 all-gather.7.cloned.1.call-start
  22.5 0.7 reshape_squeeze.13
  23.2 0.0 all-gather.9.cloned.1.call-start
  23.3 0.7 reshape_squeeze.14
  24.0 0.7 reshape_squeeze.15
  24.7 38.0 %all-gather.5.cloned.1.call-done = bf16[128,6144]{1,0:T(8,128)(2,1)} async-done(((bf16[8,6144]{1,0:T(8,128)(2,1)}), bf16[128,6144]{1,0:T(8,128)(2,1)}) %all-gather.5.cloned.1.call-update) | async-done | bytes 1572880 | tf_op jit(solution)/shard_map/all_gather | solution.py:76
  62.7 4.3 %fusion.23 = f32[128,512]{1,0:T(8,128)S(1)} fusion(bf16[128,6144]{1,0:T(8,128)(2,1)} %all-gather.5.cloned.1.call-done, bf16[4,6144,512]{2,1,0:T(8,128)(2,1)} %param.13), kind=kOutput, calls=%fused_computation.32 | convolution fusion | flops 805306368 | bytes 8126464 | tf_op jit(solution)/shard_map/dot_general | solution.py:71
  66.9 36.4 %all-gather.7.cloned.1.call-done = bf16[128,6144]{1,0:T(8,128)(2,1)} async-done(((bf16[8,6144]{1,0:T(8,128)(2,1)}), bf16[128,6144]{1,0:T(8,128)(2,1)}) %all-gather.7.cloned.1.call-update) | async-done | bytes 1572880 | tf_op jit(solution)/shard_map/all_gather | solution.py:76
  103.3 4.3 %fusion.19 = f32[128,512]{1,0:T(8,128)S(1)} fusion(bf16[128,6144]{1,0:T(8,128)(2,1)} %all-gather.7.cloned.1.call-done, bf16[4,6144,512]{2,1,0:T(8,128)(2,1)} %param.13), kind=kOutput, calls=%fused_computation.28 | convolution fusion | flops 805306368 | bytes 8126464 | tf_op jit(solution)/shard_map/dot_general | solution.py:71
  107.6 4.0 %fusion.59 = bf16[128,512]{1,0:T(8,128)(2,1)S(1)} fusion(bf16[128,6144]{1,0:T(8,128)(2,1)S(1)} %copy-done.6, bf16[4,6144,512]{2,1,0:T(8,128)(2,1)} %param.14, f32[128,512]{1,0:T(8,128)S(1)} %fusion.23), kind=kOutput, calls=%fused_computation.54 | convolution fusion | flops 805699584 | bytes 8257536 | tf_op jit(solution)/shard_map/dot_general | solution.py:72
  111.6 3.8 %fusion.56 = bf16[128,512]{1,0:T(8,128)(2,1)S(1)} fusion(bf16[128,6144]{1,0:T(8,128)(2,1)S(1)} %copy-done.8, bf16[4,6144,512]{2,1,0:T(8,128)(2,1)} %param.14, f32[128,512]{1,0:T(8,128)S(1)} %fusion.19), kind=kOutput, calls=%fused_computation.53 | convolution fusion | flops 805699584 | bytes 8257536 | tf_op jit(solution)/shard_map/dot_general | solution.py:72
  115.5 28.5 %all-gather.9.cloned.1.call-done = bf16[128,6144]{1,0:T(8,128)(2,1)} async-done(((bf16[8,6144]{1,0:T(8,128)(2,1)}), bf16[128,6144]{1,0:T(8,128)(2,1)}) %all-gather.9.cloned.1.call-update) | async-done | bytes 1572880 | tf_op jit(solution)/shard_map/all_gather | solution.py:76
  144.0 4.4 %fusion.15 = f32[128,512]{1,0:T(8,128)S(1)} fusion(bf16[128,6144]{1,0:T(8,128)(2,1)} %all-gather.9.cloned.1.call-done, bf16[4,6144,512]{2,1,0:T(8,128)(2,1)} %param.13), kind=kOutput, calls=%fused_computation.24 | convolution fusion | flops 805306368 | bytes 8126464 | tf_op jit(solution)/shard_map/dot_general | solution.py:71
  148.4 3.8 %fusion.53 = bf16[128,512]{1,0:T(8,128)(2,1)S(1)} fusion(bf16[128,6144]{1,0:T(8,128)(2,1)S(1)} %copy-done.9, bf16[4,6144,512]{2,1,0:T(8,128)(2,1)} %param.14, f32[128,512]{1,0:T(8,128)S(1)} %fusion.15), kind=kOutput, calls=%fused_computation.52 | convolution fusion | flops 805699584 | bytes 8257536 | tf_op jit(solution)/shard_map/dot_general | solution.py:72
  152.2 3.9 %fusion = bf16[16,2,1,4,6144]{4,0,3,1,2:T(8,128)(2,1)S(1)} fusion(bf16[4,512,6144]{2,1,0:T(8,128)(2,1)} %param.15, bf16[16,2,4,512]{3,2,1,0:T(4,128)(2,1)S(1)} %reshape.110), kind=kOutput, calls=%fused_computation.7 | convolution fusion | flops 806092800 | bytes 7995392 | tf_op jit(solution)/shard_map/dot_general | solution.py:80
  156.1 3.8 %fusion.1 = bf16[16,2,1,4,6144]{4,0,3,1,2:T(8,128)(2,1)S(1)} fusion(bf16[4,512,6144]{2,1,0:T(8,128)(2,1)} %param.15, bf16[16,2,4,512]{3,2,1,0:T(4,128)(2,1)S(1)} %reshape.111), kind=kOutput, calls=%fused_computation.8 | convolution fusion | flops 806092800 | bytes 7995392 | tf_op jit(solution)/shard_map/dot_general | solution.py:80
  159.9 5.0 %fusion.2 = bf16[16,2,1,4,6144]{4,0,3,1,2:T(8,128)(2,1)} fusion(bf16[4,512,6144]{2,1,0:T(8,128)(2,1)} %param.15, bf16[16,2,4,512]{3,2,1,0:T(4,128)(2,1)S(1)} %reshape.112), kind=kOutput, calls=%fused_computation.9 | convolution fusion | flops 806092800 | bytes 7995392 | tf_op jit(solution)/shard_map/dot_general | solution.py:80
  164.9 20.2 %all-gather.11.cloned.1.call-done = bf16[128,6144]{1,0:T(8,128)(2,1)} async-done(((bf16[8,6144]{1,0:T(8,128)(2,1)}), bf16[128,6144]{1,0:T(8,128)(2,1)}) %all-gather.11.cloned.1.call-update) | async-done | bytes 1572880 | tf_op jit(solution)/shard_map/all_gather | solution.py:76
  185.1 4.4 %fusion.11 = f32[128,512]{1,0:T(8,128)S(1)} fusion(bf16[128,6144]{1,0:T(8,128)(2,1)} %all-gather.11.cloned.1.call-done, bf16[4,6144,512]{2,1,0:T(8,128)(2,1)} %param.13), kind=kOutput, calls=%fused_computation.20 | convolution fusion | flops 805306368 | bytes 8126464 | tf_op jit(solution)/shard_map/dot_general | solution.py:71
  189.4 3.8 %fusion.50 = bf16[128,512]{1,0:T(8,128)(2,1)S(1)} fusion(bf16[128,6144]{1,0:T(8,128)(2,1)S(1)} %copy-done.7, bf16[4,6144,512]{2,1,0:T(8,128)(2,1)} %param.14, f32[128,512]{1,0:T(8,128)S(1)} %fusion.11), kind=kOutput, calls=%fused_computation.51 | convolution fusion | flops 805699584 | bytes 8257536 | tf_op jit(solution)/shard_map/dot_general | solution.py:72
  193.3 3.9 %fusion.3 = bf16[16,2,1,4,6144]{4,0,3,1,2:T(8,128)(2,1)S(1)} fusion(bf16[4,512,6144]{2,1,0:T(8,128)(2,1)} %param.15, bf16[16,2,4,512]{3,2,1,0:T(4,128)(2,1)S(1)} %reshape.113), kind=kOutput, calls=%fused_computation.10 | convolution fusion | flops 806092800 | bytes 7995392 | tf_op jit(solution)/shard_map/dot_general | solution.py:80
  197.2 1.0 pad_maximum_fusion
  198.2 3.0 copy.83
  201.3 6.4 %all-to-all-start.1 = ((bf16[16,2,4,4,6144]{4,0,3,2,1:T(8,128)(2,1)}), bf16[16,2,4,4,6144]{4,0,3,2,1:T(8,128)(2,1)}, u32[]{:S(2)}, u32[]{:S(2)}) async-start(bf16[16,2,4,4,6144]{4,0,3,2,1:T(8,128)(2,1)} %copy.83), calls=%async_computation.1 | async-start | bytes 12582912 | tf_op jit(solution)/shard_map/all_to_all | solution.py:83
  207.8 0.1 reduce_sum.39
  207.9 0.1 copy.76
  207.9 0.1 copy.77
  208.0 0.1 reshape.139
  208.1 19.6 %all_gather.21 = f32[6144,8]{0,1:T(8,128)S(1)} all-gather(f32[384,8]{0,1:T(8,128)S(1)} %copy-done.3), channel_id=1, replica_groups=mesh['dp'=16,'expert'=2] {'dp'}, dimensions={0}, use_global_device_ids=true | all-gather | bytes 208896 | tf_op jit(solution)/shard_map/all_gather | solution.py:24
  227.8 0.6 fusion.63
  228.4 0.7 gather_fusion
  229.0 0.1 reshape.142
  229.1 0.1 broadcast_subtract_fusion.1
  229.2 0.1 pad_maximum_fusion.1
  229.3 0.1 copy.78
  229.4 0.1 copy.72
  229.4 0.1 select_reduce_fusion
  229.5 17.6 %all_gather.22 = f32[128,32]{1,0:T(8,128)S(1)} all-gather(f32[8,32]{1,0:T(8,128)S(1)} %select_reduce_fusion), channel_id=1, replica_groups=mesh['dp'=16,'expert'=2] {'dp'}, dimensions={0}, use_global_device_ids=true | all-gather | bytes 17408 | tf_op jit(solution)/shard_map/all_gather | solution.py:88
  247.1 31.1 %all-to-all-done.1 = bf16[16,2,4,4,6144]{4,0,3,2,1:T(8,128)(2,1)} async-done(((bf16[16,2,4,4,6144]{4,0,3,2,1:T(8,128)(2,1)}), bf16[16,2,4,4,6144]{4,0,3,2,1:T(8,128)(2,1)}, u32[]{:S(2)}, u32[]{:S(2)}) %all-to-all-start.1) | async-done | bytes 6291488 | tf_op jit(solution)/shard_map/all_to_all | solution.py:83
  278.2 13.7 %fusion.4 = bf16[128,6144]{1,0:T(8,128)(2,1)} fusion(bf16[16,32,6144]{2,0,1:T(8,128)(2,1)} %bitcast.26, f32[128,32]{1,0:T(8,128)S(1)} %all_gather.22), kind=kOutput, calls=%fused_computation.11 | convolution fusion | flops 302776320 | bytes 7880704 | tf_op jit(solution)/shard_map/itc,icd->itd/dot_general | solution.py:91
  292.0 0.1 copy.85
  292.0 0.1 copy.88
  292.1 0.1 copy.89
  292.2 0.1 reshape.144
  292.3 19.6 %all_gather.27 = f32[6144,8]{0,1:T(8,128)S(1)} all-gather(f32[384,8]{0,1:T(8,128)S(1)} %copy-done.4), channel_id=1, replica_groups=mesh['dp'=16,'expert'=2] {'dp'}, dimensions={0}, use_global_device_ids=true | all-gather | bytes 208896 | tf_op jit(solution)/shard_map/all_gather | solution.py:25
  311.9 37.5 %reduce-scatter.2.cloned.1.call-done = bf16[8,6144]{1,0:T(8,128)(2,1)} async-done(((bf16[128,6144]{1,0:T(8,128)(2,1)}), bf16[8,6144]{1,0:T(8,128)(2,1)}) %reduce-scatter.2.cloned.1.call-update) | async-done | bytes 98320 | tf_op jit(solution)/shard_map/reduce_scatter | solution.py:92
  349.5 1.7 multiply_reduce_fusion
  351.2 1.5 fusion.65
  352.7 0.7 gather_fusion.1
  353.3 0.1 reshape.147
  353.4 0.1 broadcast_subtract_fusion
  353.5 0.1 copy.90
  353.6 0.1 copy.91
  353.7 0.6 pad_maximum_fusion.2
  (42 shorter events, 0.5 us)
Async XLA Ops:
  7.2 55.5 %all-gather.5.cloned.1.call-start = ((), (), s32[]{:S(2)}) async-start(), calls=%async_computation.3 | async-start | bytes 1671168 | tf_op jit(solution)/shard_map/all_gather | solution.py:76
  22.5 80.9 %all-gather.7.cloned.1.call-start = ((), (), s32[]{:S(2)}) async-start(), calls=%async_computation.4 | async-start | bytes 1671168 | tf_op jit(solution)/shard_map/all_gather | solution.py:76
  23.2 120.8 %all-gather.9.cloned.1.call-start = ((), (), s32[]{:S(2)}) async-start(), calls=%async_computation.5 | async-start | bytes 1671168 | tf_op jit(solution)/shard_map/all_gather | solution.py:76
  24.0 161.1 %all-gather.11.cloned.1.call-start = ((), (), s32[]{:S(2)}) async-start(), calls=%async_computation.6 | async-start | bytes 1671168 | tf_op jit(solution)/shard_map/all_gather | solution.py:76
  66.9 40.7 %copy-start.6 = (bf16[128,6144]{1,0:T(8,128)(2,1)S(1)}, bf16[128,6144]{1,0:T(8,128)(2,1)}, u32[]{:S(2)}) copy-start(bf16[128,6144]{1,0:T(8,128)(2,1)} %all-gather.5.cloned.1.call-done) | copy-start | bytes 4718596
  107.6 4.0 %copy-start.8 = (bf16[128,6144]{1,0:T(8,128)(2,1)S(1)}, bf16[128,6144]{1,0:T(8,128)(2,1)}, u32[]{:S(2)}) copy-start(bf16[128,6144]{1,0:T(8,128)(2,1)} %all-gather.7.cloned.1.call-done) | copy-start | bytes 4718596
  144.0 4.4 %copy-start.9 = (bf16[128,6144]{1,0:T(8,128)(2,1)S(1)}, bf16[128,6144]{1,0:T(8,128)(2,1)}, u32[]{:S(2)}) copy-start(bf16[128,6144]{1,0:T(8,128)(2,1)} %all-gather.9.cloned.1.call-done) | copy-start | bytes 4718596
  185.1 4.4 %copy-start.7 = (bf16[128,6144]{1,0:T(8,128)(2,1)S(1)}, bf16[128,6144]{1,0:T(8,128)(2,1)}, u32[]{:S(2)}) copy-start(bf16[128,6144]{1,0:T(8,128)(2,1)} %all-gather.11.cloned.1.call-done) | copy-start | bytes 4718596
  193.3 3.9 %copy-start.2 = (bf16[16,2,1,4,6144]{4,0,3,1,2:T(8,128)(2,1)S(1)}, bf16[16,2,1,4,6144]{4,0,3,1,2:T(8,128)(2,1)}, u32[]{:S(2)}) copy-start(bf16[16,2,1,4,6144]{4,0,3,1,2:T(8,128)(2,1)} %fusion.2) | copy-start | bytes 4718596
  201.3 6.8 %copy-start.3 = (f32[384,8]{0,1:T(8,128)S(1)}, f32[384,8]{0,1:T(8,128)}, u32[]{:S(2)}) copy-start(f32[384,8]{0,1:T(8,128)} %param.11) | copy-start | bytes 36868
  201.3 26.5 %copy-start.1 = (bf16[8,6144]{1,0:T(8,128)(2,1)S(1)}, bf16[8,6144]{1,0:T(8,128)(2,1)}, u32[]{:S(2)}) copy-start(bf16[8,6144]{1,0:T(8,128)(2,1)} %param.10) | copy-start | bytes 294916
  201.3 76.9 %all-to-all-start.1 = ((bf16[16,2,4,4,6144]{4,0,3,2,1:T(8,128)(2,1)}), bf16[16,2,4,4,6144]{4,0,3,2,1:T(8,128)(2,1)}, u32[]{:S(2)}, u32[]{:S(2)}) async-start(bf16[16,2,4,4,6144]{4,0,3,2,1:T(8,128)(2,1)} %copy.83), calls=%async_computation.1 | async-start | bytes 12582912 | tf_op jit(solution)/shard_map/all_to_all | solution.py:83
  207.7 141.8 %reduce-scatter.2.cloned.1.call-start = ((), (), s32[]{:S(2)}) async-start(), calls=%async_computation.7 | async-start | bytes 1671168 | tf_op jit(solution)/shard_map/reduce_scatter | solution.py:92
  278.2 13.7 %copy-start.5 = (s32[8,2]{0,1:T(2,128)S(1)}, s32[8,2]{0,1:T(2,128)}, u32[]{:S(2)}) copy-start(s32[8,2]{0,1:T(2,128)} %param.17) | copy-start | bytes 196
  278.2 14.1 %copy-start.4 = (f32[384,8]{0,1:T(8,128)S(1)}, f32[384,8]{0,1:T(8,128)}, u32[]{:S(2)}) copy-start(f32[384,8]{0,1:T(8,128)} %param.12) | copy-start | bytes 36868
  352.7 1.6 copy-start
Sparse Core Ops, SparseCore 0:
  22.6 40.0 all-gather.4
  64.9 38.3 all-gather.6
  105.6 38.3 all-gather.8
  146.7 38.2 all-gather.10
  292.1 57.3 reduce-scatter.1
where the time goes:
time: 361 us
  waiting for transfers between devices  192 us (53%)
  blocking collectives  67.5 us (19%)
  matrix products  66.4 us (18%)
  between operations  14 us (4%)
  local copies, waits for them, and re-layouts  9.48 us (3%)
  starting transfers between devices  6.61 us (2%)
  other arithmetic  5.05 us (1%)
    all_gather x4, waiting for transfers between devices, on_device(): lax.all_gather(arriving, 'dp', axis=0, tiled=True)  123 us
    reduce_scatter x1, waiting for transfers between devices, on_device(): lax.psum_scatter(token_terms.reshape(rows_dp * tok_count, width).astype(j...  37.5 us
    all_to_all x1, waiting for transfers between devices, on_device(): lax.all_to_all(stacked.astype(jnp.bfloat16), 'expert', split_axis=1, conc...  31.1 us
    all_gather x1, blocking collectives, on_device(): lax.all_gather(router_now, 'dp', axis=0, tiled=True)  19.6 us
    all_gather x1, blocking collectives, on_device(): lax.all_gather(router_next, 'dp', axis=0, tiled=True)  19.6 us
    all_gather x1, blocking collectives, on_device(): lax.all_gather(combine, 'dp', axis=0, tiled=True)  17.6 us
    dot_general x4, matrix products, activate(): gate = jnp.dot(piece, w_gate[local], preferred_element_type=jnp.float32)  17.3 us
    dot_general x4, matrix products, on_device(): jnp.dot(hidden_list[local], w_down[local], preferred_element_type=jnp.flo...  16.5 us
  transfers between devices with their start and end apart: 6, of which 6 were waited for; matrix products, arithmetic and copies ran while one was open for 12% of the time, Pallas kernels for 0%

commit v1 on v0

v1 whole, which is shorter than its diff:
```python
import functools

import jax
import jax.numpy as jnp
from jax import lax
from jax.experimental import pallas as pl
from jax.experimental.pallas import tpu as pltpu
from jax.sharding import PartitionSpec as P

epsilon = 1e-05
BOTH = ("dp", "expert")
ROOM = 1 << 21


def rms_normed(values):
    return values * lax.rsqrt(jnp.mean(values * values, axis=-1, keepdims=True) + epsilon)


def pair_weights(logits, chosen):
    picked = jnp.take_along_axis(logits, chosen, axis=1)
    first = jax.nn.sigmoid(picked[:, 0] - picked[:, 1])
    return jnp.stack([first, 1.0 - first], axis=1)


def ffn_kernel(
    in_slots, out_slots, columns, x_ref, share_ref, gate_hbm, up_hbm, down_hbm, out_ref,
    in_buf, down_buf, hidden, in_sem, down_sem,
):
    experts, width, units = gate_hbm.shape
    chunks = width // columns

    def in_copies(e):
        slot = lax.rem(e, in_slots)
        return [
            pltpu.make_async_copy(w.at[e], in_buf.at[slot, i], in_sem.at[slot, i])
            for i, w in enumerate((gate_hbm, up_hbm))
        ]

    def down_copy(n):
        slot = lax.rem(n, out_slots)
        at = pl.ds(pl.multiple_of(n * columns, 128), columns)
        return pltpu.make_async_copy(
            down_hbm.at[:, :, at], down_buf.at[slot], down_sem.at[slot]
        )

    for e in range(min(in_slots, experts)):
        for copy in in_copies(e):
            copy.start()
    for n in range(min(out_slots, chunks)):
        down_copy(n).start()

    def first(e, carry):
        slot = lax.rem(e, in_slots)
        gate_copy, up_copy = in_copies(e)
        gate_copy.wait()
        gate = jnp.dot(x_ref[...], in_buf[slot, 0], preferred_element_type=jnp.float32)
        up_copy.wait()
        upward = jnp.dot(x_ref[...], in_buf[slot, 1], preferred_element_type=jnp.float32)
        value = gate / (1.0 + jnp.exp(-gate)) * upward * share_ref[e]
        hidden[:, pl.ds(pl.multiple_of(e * units, 128), units)] = value.astype(jnp.bfloat16)

        @pl.when(e + in_slots < experts)
        def _():
            for copy in in_copies(e + in_slots):
                copy.start()

        return carry

    lax.fori_loop(0, experts, first, 0)

    def second(n, carry):
        slot = lax.rem(n, out_slots)
        down_copy(n).wait()
        weights = down_buf[slot].reshape(experts * units, columns)
        total = jnp.dot(hidden[...], weights, preferred_element_type=jnp.float32)
        out_ref[:, pl.ds(pl.multiple_of(n * columns, 128), columns)] = total.astype(jnp.bfloat16)

        @pl.when(n + out_slots < chunks)
        def _():
            down_copy(n + out_slots).start()

        return carry

    lax.fori_loop(0, chunks, second, 0)


def local_experts(everyone, share, w_gate, w_up, w_down):
    experts, width, units = w_gate.shape
    rows = everyone.shape[0]
    if rows * width > ROOM:
        total = jnp.zeros((rows, width), jnp.float32)
        for e in range(experts):
            gate = jnp.dot(everyone, w_gate[e], preferred_element_type=jnp.float32)
            upward = jnp.dot(everyone, w_up[e], preferred_element_type=jnp.float32)
            value = gate / (1.0 + jnp.exp(-gate)) * upward * share[e]
            value = value.astype(jnp.bfloat16)
            total = total + jnp.dot(value, w_down[e], preferred_element_type=jnp.float32)
        return total.astype(jnp.bfloat16)
    columns, in_slots, out_slots = 768, 3, 4
    vmem = pl.BlockSpec(memory_space=pltpu.VMEM)
    hbm = pl.BlockSpec(memory_space=pltpu.HBM)
    return pl.pallas_call(
        functools.partial(ffn_kernel, in_slots, out_slots, columns),
        out_shape=jax.ShapeDtypeStruct((rows, width), jnp.bfloat16),
        in_specs=[vmem, vmem, hbm, hbm, hbm],
        out_specs=vmem,
        scratch_shapes=[
            pltpu.VMEM((in_slots, 2, width, units), jnp.bfloat16),
            pltpu.VMEM((out_slots, experts, units, columns), jnp.bfloat16),
            pltpu.VMEM((rows, experts * units), jnp.bfloat16),
            pltpu.SemaphoreType.DMA((in_slots, 2)),
            pltpu.SemaphoreType.DMA((out_slots,)),
        ],
        compiler_params=pltpu.CompilerParams(vmem_limit_bytes=67043328),
        cost_estimate=pl.CostEstimate(
            flops=6 * rows * experts * width * units,
            bytes_accessed=6 * experts * width * units,
            transcendentals=0,
        ),
    )(everyone, share, w_gate, w_up, w_down)


def on_device(tokens, router_now, router_next, w_gate, w_up, w_down, expert_ids, next_ids):
    experts, width, units = w_gate.shape
    count = router_now.shape[1]
    resid = tokens.astype(jnp.float32)
    normed = rms_normed(resid)
    everyone = lax.all_gather(normed.astype(jnp.bfloat16), BOTH, axis=0, tiled=True)
    rows = everyone.shape[0]
    routers = jnp.concatenate([router_now.T, router_next.T], axis=0)
    routers = lax.all_gather(routers, "dp", axis=1, tiled=True)
    whole_now, whole_next = routers[:count], routers[count:]
    exact = functools.partial(
        lax.dot_general,
        dimension_numbers=(((1,), (1,)), ((), ())),
        precision=lax.Precision.HIGHEST,
        preferred_element_type=jnp.float32,
    )
    logits = exact(normed, whole_now)
    weights = pair_weights(logits, expert_ids)
    named = expert_ids[:, :, None] == jnp.arange(count, dtype=jnp.int32)[None, None, :]
    table = jnp.sum(jnp.where(named, weights[:, :, None], 0.0), axis=1)
    table = lax.all_gather(table, BOTH, axis=0, tiled=True)
    share = lax.dynamic_slice_in_dim(table, lax.axis_index("expert") * experts, experts, axis=1)
    share = share.T[:, :, None]

    partial = local_experts(everyone, share, w_gate, w_up, w_down)
    mixture = lax.psum_scatter(partial, BOTH, scatter_dimension=0, tiled=True)
    summed = resid + mixture.astype(jnp.float32)
    layer_out = summed.astype(jnp.bfloat16)
    next_logits = exact(rms_normed(summed), whole_next)
    return (layer_out, next_logits, pair_weights(next_logits, next_ids))


def solution(mesh):
    in_specs = (
        P(BOTH, None),
        P("dp", None),
        P("dp", None),
        P("expert", None, "dp"),
        P("expert", None, "dp"),
        P("expert", "dp", None),
        P(BOTH, None),
        P(BOTH, None),
    )
    out_specs = (P(BOTH, None), P(BOTH, None), P(BOTH, None))
    return jax.shard_map(
        on_device, mesh=mesh, in_specs=in_specs, out_specs=out_specs, check_vma=False
    )
```

time: 361 us -> 252 us (0.70)
  waiting for transfers between devices: 192 us -> 97.8 us
  matrix products: 66.4 us -> 3.1 us
  Pallas kernels: 0 us -> 32.7 us
  blocking collectives: 67.5 us -> 90.1 us
  starting transfers between devices: 6.61 us -> 0.08 us
    all_gather x4 -> x1, waiting for transfers between devices: 123 us -> 0.01 us  [on_device(): lax.all_gather(normed.astype(jnp.bfloat16), BOTH, axis=0, tiled=True)]
    dot_general x16 -> x2, matrix products: 66.4 us -> 3.1 us  [the longest x1 1.62 us: on_device(): next_logits = exact(rms_normed(summed), whole_next)]
    reduce_scatter x1, waiting for transfers between devices: 37.5 us -> 97.8 us  [on_device(): mixture = lax.psum_scatter(partial, BOTH, scatter_dimension=0, tiled=True)]
    all_gather x3 -> x2, blocking collectives: 56.9 us -> 90.1 us  [the longest x1 65.7 us: on_device(): table = lax.all_gather(table, BOTH, axis=0, tiled=True)]
    pallas_call x0 -> x1, Pallas kernels: none -> 32.7 us  [local_experts(): pl.pallas_call(functools.partial(ffn_kernel, in_slots, out_slots, columns...]
    all_to_all x1 -> x0, waiting for transfers between devices: 31.1 us -> none  [on_device(): lax.all_to_all(stacked.astype(jnp.bfloat16), 'expert', split_axis=1, conc...]
    all_to_all x1 -> x0, blocking collectives: 10.6 us -> none  [on_device(): lax.all_to_all(dispatched, 'expert', split_axis=0, concat_axis=0, tiled=T...]
    all_to_all x1 -> x0, starting transfers between devices: 6.4 us -> none  [on_device(): lax.all_to_all(stacked.astype(jnp.bfloat16), 'expert', split_axis=1, conc...]
  transfers between devices with their start and end apart: 6 -> 2, of which waited for: 6 -> 1; matrix products, arithmetic and copies ran while one was open for 12% -> 4% of each run, Pallas kernels for 0% -> 0%
where the time goes in v1:
time: 252 us
  waiting for transfers between devices  97.8 us (39%)
  blocking collectives  90.1 us (36%)
  Pallas kernels  32.7 us (13%)
  between operations  14.1 us (6%)
  local copies, waits for them, and re-layouts  7.29 us (3%)
  other arithmetic  6.81 us (3%)
  matrix products  3.1 us (1%)
    reduce_scatter x1, waiting for transfers between devices, on_device(): mixture = lax.psum_scatter(partial, BOTH, scatter_dimension=0, tiled=True)  97.8 us
    all_gather x1, blocking collectives, on_device(): table = lax.all_gather(table, BOTH, axis=0, tiled=True)  65.7 us
    pallas_call x1, Pallas kernels, local_experts(): pl.pallas_call(functools.partial(ffn_kernel, in_slots, out_slots, columns...  32.7 us
    all_gather x1, blocking collectives, on_device(): routers = lax.all_gather(routers, 'dp', axis=1, tiled=True)  24.4 us
  transfers between devices with their start and end apart: 2, of which 1 were waited for; matrix products, arithmetic and copies ran while one was open for 4% of the time, Pallas kernels for 0%

profile of v1, /device:TPU:0, one launch (start us, length us, event | category | flops | bytes accessed | tf_op | source)
XLA Modules:
  0.0 252.0 jit_solution(11559998849633108371)
XLA Ops:
  7.2 0.0 all-gather.2.cloned.1.call-start
  7.2 1.1 fusion.2
  8.3 1.6 fusion.1
  9.9 0.0 all-gather.2.cloned.1.call-update
  9.9 0.0 reduce-scatter.2.cloned.1.call-start
  10.0 0.8 copy.54
  10.7 0.1 copy.57
  10.8 0.1 copy.58
  10.9 0.1 reshape.56
  11.0 0.7 pad_maximum_fusion
  11.7 24.4 %all_gather.10 = f32[16,6144]{1,0:T(8,128)S(1)} all-gather(f32[16,384]{1,0:T(8,128)S(1)} %pad_maximum_fusion), channel_id=1, replica_groups=mesh['dp'=16,'expert'=2] {'dp'}, dimensions={1}, use_global_device_ids=true | all-gather | bytes 417792 | tf_op jit(solution)/shard_map/all_gather | solution.py:131
  36.2 0.0 copy-start.1
  36.2 0.7 copy-done.1
  36.9 1.5 fusion
  38.4 0.7 gather_fusion
  39.1 0.1 reshape.59
  39.2 0.1 broadcast_subtract_fusion.1
  39.2 0.1 pad_maximum_fusion.1
  39.3 0.1 copy.59
  39.4 0.8 select_reduce_fusion
  40.2 65.7 %all_gather.11 = f32[256,8]{1,0:T(8,128)S(1)} all-gather(f32[8,8]{1,0:T(8,128)S(1)} %select_reduce_fusion), channel_id=1, replica_groups=mesh['dp'=16,'expert'=2] {'dp','expert'}, dimensions={0}, use_global_device_ids=true | all-gather | bytes 8448 | tf_op jit(solution)/shard_map/all_gather | solution.py:143
  105.8 0.1 dynamic-slice_bitcast_fusion
  105.9 2.7 %copy.61.share_ref = f32[4,256,1]{2,1,0:T(8,128)} copy(f32[4,256,1]{0,1,2:T(8,128)S(1)} %dynamic-slice_bitcast_fusion) | data formatting | bytes 8192 | tf_op jit(solution)/shard_map/broadcast_in_dim | solution.py:145
  108.6 0.0 all-gather.2.cloned.1.call-done.x_ref
  108.6 32.7 %shard_map.103 = bf16[256,6144]{1,0:T(8,128)(2,1)} custom-call(bf16[256,6144]{1,0:T(8,128)(2,1)} %all-gather.2.cloned.1.call-done.x_ref, f32[4,256,1]{2,1,0:T(8,128)} %copy.61.share_ref, bf16[4,6144,512]{2,1,0:T(8,128)(2,1)} %gate_hbm.1, bf16[4,6144,512]{2,1,0:T(8,128)(2,1)} %up_hbm.1, bf16[4,512,6144]{2,1,0:T(8,128)(2,1)} %down_hbm.1), custom_call_target="tpu_custom_call" | custom-call | flops 19327352832 | bytes 75497472 | tf_op jit(solution)/shard_map/pallas_call | solution.py:102
  141.3 0.0 reduce-scatter.2.cloned.1.call-update
  141.4 0.8 copy.62
  142.1 0.1 copy.65
  142.2 0.1 copy.66
  142.3 0.1 reshape.61
  142.4 97.8 %reduce-scatter.2.cloned.1.call-done = bf16[8,6144]{1,0:T(8,128)(2,1)} async-done(((bf16[256,6144]{1,0:T(8,128)(2,1)}), bf16[8,6144]{1,0:T(8,128)(2,1)}) %reduce-scatter.2.cloned.1.call-update) | async-done | bytes 98320 | tf_op jit(solution)/shard_map/reduce_scatter | solution.py:148
  240.2 1.7 multiply_reduce_fusion
  241.9 1.6 fusion.3
  243.5 0.0 copy-start
  243.5 0.7 gather_fusion.1
  244.2 0.1 reshape.64
  244.3 0.1 broadcast_subtract_fusion
  244.4 0.1 copy.67
  244.4 0.1 copy.68
  244.5 0.6 pad_maximum_fusion.2
  245.1 0.0 copy-done
  (8 shorter events, 0.1 us)
Async XLA Ops:
  7.2 101.5 %all-gather.2.cloned.1.call-start = ((), (), s32[]{:S(2)}) async-start(), calls=%async_computation.1 | async-start | bytes 3244032 | tf_op jit(solution)/shard_map/all_gather | solution.py:128
  9.9 230.3 %reduce-scatter.2.cloned.1.call-start = ((), (), s32[]{:S(2)}) async-start(), calls=%async_computation.2 | async-start | bytes 3244032 | tf_op jit(solution)/shard_map/reduce_scatter | solution.py:148
  36.2 0.8 copy-start.1
  243.5 1.6 copy-start
Sparse Core Ops, SparseCore 0:
  11.4 62.3 all-gather.1
  141.5 98.6 reduce-scatter.1
